TPU v7x, 256 devices: a whole 4x4x8 slice. The times are simulated.
256 devices in a mesh: tp: 8 (over z_lo, x), dp: 8 (over y, core), rep: 4 (over z_hi).
Axes of the slice: x: 4, y: 4, z: 8 (z_hi: 4, z_lo: 2; z = z_hi * 2 + z_lo), core: 2. Of those that a mesh axis runs over, the one named last changes fastest.
Arguments:
- prompts: bfloat16 [24576, 8192], P(('dp', 'rep'), 'tp'), may hold values from -6 to 6
- frozen_projection_weight: bfloat16 [2, 8192, 2048], P(None, ('dp', 'rep'), 'tp'), may hold values from -5 to 5
- lowrank_down_factor: bfloat16 [2, 8192, 64], P(None, ('dp', 'rep')), may hold values from -0.119628906 to 0.119628906
- lowrank_up_factor: bfloat16 [2, 64, 2048], P(None, None, 'tp'), may hold values from -0.59765625 to 0.59765625
- magnitude: float32 [2, 2048], P(None, 'tp'), may hold values from 0.5 to 2
Outputs:
- key_values: bfloat16 [2, 24576, 2048], P(None, ('dp', 'rep'), 'tp')
All inputs are finite; a program needn't handle non-finite values.
Results may differ from a plain program's by a relative error of at most 0.0049.
Values may be sent and summed in bfloat16 or wider, within the bound.
No kernel may reach another device: no remote copies, remote signals or barrier semaphores. Data moves between devices by JAX's collectives and lax.ppermute only.
A program may use at most 64 MiB of HBM per device.

v0:
```python
import functools
import jax
import jax.numpy as jnp
from jax import lax
from jax.sharding import Mesh
from jax.sharding import PartitionSpec as P

DP_REP = ("dp_0", "dp_1", "rep")
epsilon = 1e-06


def one_axis_at_a_time(array, axes):
    return functools.reduce(lax.psum, axes, array)


def combine_weight_rows(weight_rows, down_rows, up_matrix):
    return weight_rows.astype(jnp.float32) + jnp.dot(
        down_rows, up_matrix, preferred_element_type=jnp.float32
    )


def prefilled_shard_values(
    frozen_projection_weight, lowrank_down_factor, lowrank_up_factor, magnitude, current_layer_index
):
    combined_weight = combine_weight_rows(
        frozen_projection_weight[current_layer_index],
        lowrank_down_factor[current_layer_index],
        lowrank_up_factor[current_layer_index],
    )
    squares = one_axis_at_a_time(jnp.sum(combined_weight * combined_weight, axis=0), DP_REP)
    factor = magnitude[current_layer_index] / jnp.sqrt(squares + epsilon)
    return (combined_weight * factor).astype(jnp.bfloat16)


def local(prompts, frozen_projection_weight, lowrank_down_factor, lowrank_up_factor, magnitude):
    layer_total = frozen_projection_weight.shape[0]
    features = lax.all_gather(prompts, "tp", axis=1, tiled=True)
    outputs = []
    for current_layer_index in range(layer_total):
        prefilled_key_values = prefilled_shard_values(
            frozen_projection_weight,
            lowrank_down_factor,
            lowrank_up_factor,
            magnitude,
            current_layer_index,
        )
        result = jnp.dot(
            features,
            lax.all_gather(prefilled_key_values, DP_REP, axis=0, tiled=True),
            preferred_element_type=jnp.float32,
        )
        outputs.append(result.astype(jnp.bfloat16))
    return jnp.stack(outputs)


def solution(mesh):
    split = Mesh(
        mesh.devices.reshape(mesh.shape["tp"], 4, 2, mesh.shape["rep"]),
        ("tp", "dp_0", "dp_1", "rep"),
    )
    in_specs = (
        P(DP_REP, "tp"),
        P(None, DP_REP, "tp"),
        P(None, DP_REP, None),
        P(None, None, "tp"),
        P(None, "tp"),
    )
    out_specs = P(None, DP_REP, "tp")
    return jax.shard_map(local, mesh=split, in_specs=in_specs, out_specs=out_specs, check_vma=False)
```

profile of v0, /device:TPU:1, one launch (start us, length us, event | category | flops | bytes accessed | tf_op | source)
XLA Modules:
  0.0 308.4 jit_solution(7998691284493703192)
XLA Ops:
  6.5 0.0 all-gather.4.cloned.1.call-start
  6.5 1.2 multiply_reduce_fusion
  7.7 1.2 multiply_reduce_fusion.1
  8.9 0.8 fusion.10
  9.7 9.5 %all-reduce.1 = (f32[256]{0:T(256)S(1)}, f32[256]{0:T(256)S(1)}) all-reduce(f32[256]{0:T(256)S(1)} %get-tuple-element.13, f32[256]{0:T(256)S(1)} %get-tuple-element.15), channel_id=1, replica_groups=mesh['tp'=8,'dp_0'=4,'dp_1'=2,'rep'=4] {'dp_0'}, use_global_device_ids=true, to_apply=%region_5.0 | all-reduce | flops 512 | bytes 4096 | tf_op jit(solution)/shard_map/psum | solution.py:13
  19.2 4.8 %all-reduce.2 = (f32[256]{0:T(256)S(1)}, f32[256]{0:T(256)S(1)}) all-reduce(f32[256]{0:T(256)S(1)} %get-tuple-element.7, f32[256]{0:T(256)S(1)} %get-tuple-element.8), channel_id=1, replica_groups=mesh['tp'=8,'dp_0'=4,'dp_1'=2,'rep'=4] {'dp_1'}, use_global_device_ids=true, to_apply=%region_6.0 | all-reduce | flops 512 | bytes 4096 | tf_op jit(solution)/shard_map/psum | solution.py:13
  24.0 12.9 %all-reduce = (f32[256]{0:T(256)S(1)}, f32[256]{0:T(256)S(1)}) all-reduce(f32[256]{0:T(256)S(1)} %get-tuple-element.9, f32[256]{0:T(256)S(1)} %get-tuple-element.10), channel_id=1, replica_groups=mesh['tp'=8,'dp_0'=4,'dp_1'=2,'rep'=4] {'rep'}, use_global_device_ids=true, to_apply=%region_7.0 | all-reduce | flops 512 | bytes 4096 | tf_op jit(solution)/shard_map/psum | solution.py:13
  36.9 0.7 multiply_convert_fusion.1
  37.6 0.0 all-gather.4.cloned.1.call-update
  37.6 0.0 all-gather.6.cloned.1.call-start
  37.6 0.7 all-gather.6.cloned.1.call-update
  38.3 0.0 all-gather.8.cloned.1.call-start
  38.4 0.7 multiply_convert_fusion
  39.1 0.0 all-gather.8.cloned.1.call-update
  39.1 56.9 %all-gather.4.cloned.1.call-done = bf16[8192,256]{1,0:T(8,128)(2,1)} async-done(((bf16[256,256]{1,0:T(8,128)(2,1)}), bf16[8192,256]{1,0:T(8,128)(2,1)}) %all-gather.4.cloned.1.call-update) | async-done | bytes 4194320 | tf_op jit(solution)/shard_map/all_gather | solution.py:49
  96.0 133.1 %all-gather.6.cloned.1.call-done = bf16[768,8192]{1,0:T(8,128)(2,1)} async-done(((bf16[768,1024]{1,0:T(8,128)(2,1)}), bf16[768,8192]{1,0:T(8,128)(2,1)}) %all-gather.6.cloned.1.call-update) | async-done | bytes 12582928 | tf_op jit(solution)/shard_map/all_gather | solution.py:37
  229.1 9.3 %fusion = bf16[1,768,256]{1,2,0:T(8,128)(2,1)S(1)} fusion(bf16[8192,256]{1,0:T(8,128)(2,1)} %all-gather.4.cloned.1.call-done, bf16[768,8192]{1,0:T(8,128)(2,1)} %all-gather.6.cloned.1.call-done), kind=kOutput, calls=%fused_computation.2 | convolution fusion | flops 3221422080 | bytes 17170432 | tf_op jit(solution)/shard_map/dot_general | solution.py:47
  238.4 52.9 %all-gather.8.cloned.1.call-done = bf16[8192,256]{1,0:T(8,128)(2,1)} async-done(((bf16[256,256]{1,0:T(8,128)(2,1)}), bf16[8192,256]{1,0:T(8,128)(2,1)}) %all-gather.8.cloned.1.call-update) | async-done | bytes 4194320 | tf_op jit(solution)/shard_map/all_gather | solution.py:49
  291.3 9.3 %fusion.1 = bf16[1,768,256]{1,2,0:T(8,128)(2,1)S(1)} fusion(bf16[8192,256]{1,0:T(8,128)(2,1)} %all-gather.8.cloned.1.call-done, bf16[768,8192]{1,0:T(8,128)(2,1)} %all-gather.6.cloned.1.call-done), kind=kOutput, calls=%fused_computation.3 | convolution fusion | flops 3221422080 | bytes 17170432 | tf_op jit(solution)/shard_map/dot_general | solution.py:47
  300.7 0.1 pad_maximum_fusion
  300.8 1.2 copy.6
  (2 shorter events, 0.0 us)
Async XLA Ops:
  6.5 89.5 %all-gather.4.cloned.1.call-start = ((), (), s32[]{:S(2)}) async-start(), calls=%async_computation | async-start | bytes 4325376 | tf_op jit(solution)/shard_map/all_gather | solution.py:49
  37.6 191.5 %all-gather.6.cloned.1.call-start = ((), (), s32[]{:S(2)}) async-start(), calls=%async_computation.1 | async-start | bytes 14155776 | tf_op jit(solution)/shard_map/all_gather | solution.py:37
  38.3 253.0 %all-gather.8.cloned.1.call-start = ((), (), s32[]{:S(2)}) async-start(), calls=%async_computation.2 | async-start | bytes 4325376 | tf_op jit(solution)/shard_map/all_gather | solution.py:49
Sparse Core Ops, SparseCore 0:
  37.7 58.2 all-gather.3
  97.8 131.2 all-gather.5
  231.6 59.6 all-gather.7
where the time goes:
time: 309 us; the launch traced here: 308 us
  waiting for transfers between devices  244 us (79%)
  blocking collectives  27.2 us (9%)
  matrix products  21 us (7%)
  between operations  13.1 us (4%)
    all_gather x1, waiting for transfers between devices, local(): features = lax.all_gather(prompts, 'tp', axis=1, tiled=True)  133 us
    all_gather x2, waiting for transfers between devices, local(): lax.all_gather(prefilled_key_values, DP_REP, axis=0, tiled=True)  110 us
    psum x3, blocking collectives, one_axis_at_a_time(): return functools.reduce(lax.psum, axes, array)  27.2 us
    dot_general x2, matrix products, local(): jnp.dot(features, lax.all_gather(prefilled_key_values, DP_REP, axis=0, ti...  18.6 us
  transfers between devices with their start and end apart: 3, of which 3 were waited for; matrix products, arithmetic and copies ran while one was open for 3% of the time, Pallas kernels for 0%

commit v1 on v0

--- a/solution.py
+++ b/solution.py
@@ -46,7 +46,12 @@
         )
         result = jnp.dot(
             features,
-            lax.all_gather(prefilled_key_values, DP_REP, axis=0, tiled=True),
+            jnp.concatenate(
+                lax.all_to_all(
+                    jnp.stack([prefilled_key_values] * lax.axis_size(DP_REP)), DP_REP, 0, 0
+                ),
+                axis=0,
+            ),
             preferred_element_type=jnp.float32,
         )
         outputs.append(result.astype(jnp.bfloat16))

time: 309 us -> 346 us (1.12)
  waiting for transfers between devices: 244 us -> 263 us
  starting transfers between devices: 0.08 us -> 12.3 us
  local copies, waits for them, and re-layouts: 1.92 us -> 6.79 us
    all_to_all x0 -> x2, waiting for transfers between devices: none -> 146 us  [local(): lax.all_to_all(jnp.stack([prefilled_key_values] * lax.axis_size(DP_REP)),...]
    all_gather x2 -> x0, waiting for transfers between devices: 110 us -> none  [local(): lax.all_gather(prefilled_key_values, DP_REP, axis=0, tiled=True)]
    all_gather x1, waiting for transfers between devices: 133 us -> 117 us  [local(): features = lax.all_gather(prompts, 'tp', axis=1, tiled=True)]
    all_to_all x0 -> x2, starting transfers between devices: none -> 12.3 us  [local(): lax.all_to_all(jnp.stack([prefilled_key_values] * lax.axis_size(DP_REP)),...]
    another operation x0 -> x2, local copies, waits for them, and re-layouts: none -> 4.87 us  [local(): jnp.stack([prefilled_key_values] * lax.axis_size(DP_REP))]
  transfers between devices with their start and end apart: 3 -> 3, of which waited for: 3 -> 3; matrix products, arithmetic and copies ran while one was open for 3% -> 5% of each run, Pallas kernels for 0% -> 0%
where the time goes in v1:
time: 346 us; the launch traced here: 345 us
  waiting for transfers between devices  263 us (76%)
  blocking collectives  28.2 us (8%)
  matrix products  21 us (6%)
  between operations  13.5 us (4%)
  starting transfers between devices  12.3 us (4%)
  local copies, waits for them, and re-layouts  6.79 us (2%)
    all_to_all x2, waiting for transfers between devices, local(): lax.all_to_all(jnp.stack([prefilled_key_values] * lax.axis_size(DP_REP)),...  146 us
    all_gather x1, waiting for transfers between devices, local(): features = lax.all_gather(prompts, 'tp', axis=1, tiled=True)  117 us
    psum x3, blocking collectives, one_axis_at_a_time(): return functools.reduce(lax.psum, axes, array)  28.2 us
    dot_general x2, matrix products, local(): jnp.dot(features, jnp.concatenate(lax.all_to_all(jnp.stack([prefilled_key...  18.6 us
    all_to_all x2, starting transfers between devices, local(): lax.all_to_all(jnp.stack([prefilled_key_values] * lax.axis_size(DP_REP)),...  12.3 us
  transfers between devices with their start and end apart: 3, of which 3 were waited for; matrix products, arithmetic and copies ran while one was open for 5% of the time, Pallas kernels for 0%

profile of v1, /device:TPU:1, one launch (start us, length us, event | category | flops | bytes accessed | tf_op | source)
XLA Modules:
  0.0 345.3 jit_solution(5600731911941736502)
XLA Ops:
  6.5 0.0 all-gather.2.cloned.1.call-start
  6.5 0.7 all-gather.2.cloned.1.call-update
  7.3 1.2 multiply_reduce_fusion
  8.4 1.2 multiply_reduce_fusion.1
  9.6 9.5 %all-reduce.1 = (f32[256]{0:T(256)S(1)}, f32[256]{0:T(256)S(1)}) all-reduce(f32[256]{0:T(256)S(1)} %get-tuple-element.13, f32[256]{0:T(256)S(1)} %get-tuple-element.15), channel_id=1, replica_groups=mesh['tp'=8,'dp_0'=4,'dp_1'=2,'rep'=4] {'dp_0'}, use_global_device_ids=true, to_apply=%region_5.0 | all-reduce | flops 512 | bytes 4096 | tf_op jit(solution)/shard_map/psum | solution.py:13
  19.2 4.8 %all-reduce.2 = (f32[256]{0:T(256)S(1)}, f32[256]{0:T(256)S(1)}) all-reduce(f32[256]{0:T(256)S(1)} %get-tuple-element.7, f32[256]{0:T(256)S(1)} %get-tuple-element.8), channel_id=1, replica_groups=mesh['tp'=8,'dp_0'=4,'dp_1'=2,'rep'=4] {'dp_1'}, use_global_device_ids=true, to_apply=%region_6.0 | all-reduce | flops 512 | bytes 4096 | tf_op jit(solution)/shard_map/psum | solution.py:13
  24.0 13.9 %all-reduce = (f32[256]{0:T(256)S(1)}, f32[256]{0:T(256)S(1)}) all-reduce(f32[256]{0:T(256)S(1)} %get-tuple-element.9, f32[256]{0:T(256)S(1)} %get-tuple-element.10), channel_id=1, replica_groups=mesh['tp'=8,'dp_0'=4,'dp_1'=2,'rep'=4] {'rep'}, use_global_device_ids=true, to_apply=%region_7.0 | all-reduce | flops 512 | bytes 4096 | tf_op jit(solution)/shard_map/psum | solution.py:13
  37.9 0.8 fusion.10
  38.7 2.4 stack.12
  41.1 6.1 %all-to-all-start.1 = ((bf16[32,256,256]{2,1,0:T(8,128)(2,1)}), bf16[32,256,256]{2,1,0:T(8,128)(2,1)}, u32[]{:S(2)}, u32[]{:S(2)}) async-start(bf16[32,256,256]{2,1,0:T(8,128)(2,1)} %stack.12), calls=%async_computation.1 | async-start | bytes 8388608 | tf_op jit(solution)/shard_map/all_to_all | solution.py:50
  47.3 140.6 %all-to-all-done.1 = bf16[32,256,256]{2,1,0:T(8,128)(2,1)} async-done(((bf16[32,256,256]{2,1,0:T(8,128)(2,1)}), bf16[32,256,256]{2,1,0:T(8,128)(2,1)}, u32[]{:S(2)}, u32[]{:S(2)}) %all-to-all-start.1) | async-done | bytes 4194336 | tf_op jit(solution)/shard_map/all_to_all | solution.py:50
  187.9 2.4 stack.10
  190.3 6.2 %all-to-all-start = ((bf16[32,256,256]{2,1,0:T(8,128)(2,1)}), bf16[32,256,256]{2,1,0:T(8,128)(2,1)}, u32[]{:S(2)}, u32[]{:S(2)}) async-start(bf16[32,256,256]{2,1,0:T(8,128)(2,1)} %stack.10), calls=%async_computation | async-start | bytes 8388608 | tf_op jit(solution)/shard_map/all_to_all | solution.py:50
  196.5 117.0 %all-gather.2.cloned.1.call-done = bf16[768,8192]{1,0:T(8,128)(2,1)} async-done(((bf16[768,1024]{1,0:T(8,128)(2,1)}), bf16[768,8192]{1,0:T(8,128)(2,1)}) %all-gather.2.cloned.1.call-update) | async-done | bytes 12582928 | tf_op jit(solution)/shard_map/all_gather | solution.py:37
  313.5 9.3 %fusion.1 = bf16[1,768,256]{1,2,0:T(8,128)(2,1)S(1)} fusion(bf16[8192,256]{1,0:T(8,128)(2,1)} %bitcast.11, bf16[768,8192]{1,0:T(8,128)(2,1)} %all-gather.2.cloned.1.call-done), kind=kOutput, calls=%fused_computation.3 | convolution fusion | flops 3221422080 | bytes 17170432 | tf_op jit(solution)/shard_map/dot_general | solution.py:47
  322.9 5.0 %all-to-all-done = bf16[32,256,256]{2,1,0:T(8,128)(2,1)} async-done(((bf16[32,256,256]{2,1,0:T(8,128)(2,1)}), bf16[32,256,256]{2,1,0:T(8,128)(2,1)}, u32[]{:S(2)}, u32[]{:S(2)}) %all-to-all-start) | async-done | bytes 4194336 | tf_op jit(solution)/shard_map/all_to_all | solution.py:50
  327.8 9.3 %fusion = bf16[1,768,256]{1,2,0:T(8,128)(2,1)S(1)} fusion(bf16[8192,256]{1,0:T(8,128)(2,1)} %bitcast.4, bf16[768,8192]{1,0:T(8,128)(2,1)} %all-gather.2.cloned.1.call-done), kind=kOutput, calls=%fused_computation.2 | convolution fusion | flops 3221422080 | bytes 17170432 | tf_op jit(solution)/shard_map/dot_general | solution.py:47
  337.2 0.1 pad_maximum_fusion
  337.3 1.2 copy.6
  (3 shorter events, 0.1 us)
Async XLA Ops:
  6.5 307.0 %all-gather.2.cloned.1.call-start = ((), (), s32[]{:S(2)}) async-start(), calls=%async_computation.2 | async-start | bytes 14155776 | tf_op jit(solution)/shard_map/all_gather | solution.py:37
  41.1 146.8 %all-to-all-start.1 = ((bf16[32,256,256]{2,1,0:T(8,128)(2,1)}), bf16[32,256,256]{2,1,0:T(8,128)(2,1)}, u32[]{:S(2)}, u32[]{:S(2)}) async-start(bf16[32,256,256]{2,1,0:T(8,128)(2,1)} %stack.12), calls=%async_computation.1 | async-start | bytes 8388608 | tf_op jit(solution)/shard_map/all_to_all | solution.py:50
  190.3 137.5 %all-to-all-start = ((bf16[32,256,256]{2,1,0:T(8,128)(2,1)}), bf16[32,256,256]{2,1,0:T(8,128)(2,1)}, u32[]{:S(2)}, u32[]{:S(2)}) async-start(bf16[32,256,256]{2,1,0:T(8,128)(2,1)} %stack.10), calls=%async_computation | async-start | bytes 8388608 | tf_op jit(solution)/shard_map/all_to_all | solution.py:50
Sparse Core Ops, SparseCore 0:
  9.1 304.3 all-gather.1
